TPU v7x, 512 devices: a whole 4x4x16 slice. The times are simulated.
512 devices in a mesh: dp: 8 (over z_lo), row: 16 (over z_hi, x, core), col: 4 (over y).
Axes of the slice: x: 4, y: 4, z: 16 (z_hi: 2, z_lo: 8; z = z_hi * 8 + z_lo), core: 2. Of those that a mesh axis runs over, the one named last changes fastest.
Arguments:
- expand_gradient: bfloat16 [8, 4096, 5120], P('dp', 'row', 'col'), may hold values from -24 to 24, as said below
- expand_master: float32 [4096, 5120], P(('row', 'dp'), 'col'), may hold values from -0.12 to 0.12
- expand_rows: float32 [4096], P(('row', 'dp')), may hold values from 0.01 to 1
- expand_columns: float32 [5120], P('col'), may hold values from 0.01 to 1
- contract_gradient: bfloat16 [8, 5120, 4096], P('dp', 'row', 'col'), may hold values from -24 to 24, as said below
- contract_master: float32 [5120, 4096], P(('row', 'dp'), 'col'), may hold values from -0.12 to 0.12
- contract_rows: float32 [5120], P(('row', 'dp')), may hold values from 0.01 to 1
- contract_columns: float32 [4096], P('col'), may hold values from 0.01 to 1
- attend_gradient: bfloat16 [8, 4096, 4096], P('dp', 'row', 'col'), may hold values from -24 to 24, as said below
- attend_master: float32 [4096, 4096], P(('row', 'dp'), 'col'), may hold values from -0.12 to 0.12
- attend_rows: float32 [4096], P(('row', 'dp')), may hold values from 0.01 to 1
- attend_columns: float32 [4096], P('col'), may hold values from 0.01 to 1
Outputs:
- expand_updated: float32 [4096, 5120], P(('row', 'dp'), 'col')
- expand_weights: bfloat16 [4096, 5120], P('row', 'col')
- expand_rows_next: float32 [4096], P(('row', 'dp'))
- expand_columns_next: float32 [5120], P('col')
- expand_step: float32 [4096, 5120], P(('row', 'dp'), 'col')
- contract_updated: float32 [5120, 4096], P(('row', 'dp'), 'col')
- contract_weights: bfloat16 [5120, 4096], P('row', 'col')
- contract_rows_next: float32 [5120], P(('row', 'dp'))
- contract_columns_next: float32 [4096], P('col')
- contract_step: float32 [5120, 4096], P(('row', 'dp'), 'col')
- attend_updated: float32 [4096, 4096], P(('row', 'dp'), 'col')
- attend_weights: bfloat16 [4096, 4096], P('row', 'col')
- attend_rows_next: float32 [4096], P(('row', 'dp'))
- attend_columns_next: float32 [4096], P('col')
- attend_step: float32 [4096, 4096], P(('row', 'dp'), 'col')
Inputs may be any that keep to these rules, and one draw needn't show every extreme that they name: `expand_gradient`: each replica's gradient, of any scale from entry to entry. `contract_gradient`: each replica's gradient, of any scale from entry to entry. `attend_gradient`: each replica's gradient, of any scale from entry to entry.
All inputs are finite; a program needn't handle non-finite values.
Results may differ from a plain program's by a relative error of at most 0.0004.
Values may be sent and summed in bfloat16 or wider, within the bound.
A program may use at most 64 MiB of HBM per device.

v0:
```python
import jax
import jax.numpy as jnp
from jax import lax
from jax.sharding import Mesh
from jax.sharding import PartitionSpec as P

ROW = ("row_0", "row_1", "row_2")
DP_ROW = ("dp", "row_0", "row_1", "row_2")
DP_ROW_COL = ("dp", "row_0", "row_1", "row_2", "col")
ROW_DP = ("row_0", "row_1", "row_2", "dp")
tiny_square = 1e-30
decay_rate = 0.9
learn_rate = 0.01


def in_order(blocks, dim):
    blocks = jnp.moveaxis(blocks, 0, dim)
    lengths = blocks.shape
    return blocks.reshape(*lengths[:dim], lengths[dim] * lengths[dim + 1], *lengths[dim + 2 :])


def from_everyone(shard, axis):
    copies = jnp.broadcast_to(shard, (lax.axis_size(axis), *shard.shape))
    return lax.all_to_all(copies, axis, split_axis=0, concat_axis=0, tiled=True)


def collect(shard, axis, dim):
    return in_order(from_everyone(shard, axis), dim)


def taken_together(shard, axis):
    everything = from_everyone(shard, axis)
    return jnp.sum(everything, axis=0)


def packed_total(arrays, axis):
    ends = [0]
    for a in arrays:
        ends.append(ends[-1] + a.size)
    subtotal = taken_together(jnp.concatenate([a.ravel() for a in arrays]), axis)
    return tuple((subtotal[b:e].reshape(a.shape) for a, b, e in zip(arrays, ends, ends[1:])))


def one_axis_at_a_time(shard, axes):
    for axis in axes:
        shard = lax.psum(shard, axis)
    return shard


def finish(update_raw, clip_total, master, full_size):
    clip_scale = jnp.maximum(1.0, jnp.sqrt(clip_total / full_size))
    step_taken = update_raw / clip_scale
    updated = master - learn_rate * step_taken
    weights = collect(updated.astype(jnp.bfloat16), "dp", 0)
    return (updated, weights, step_taken)


def reduce_gradient(gradient, dp_count):
    received = lax.all_to_all(gradient, "dp", split_axis=1, concat_axis=0, tiled=True)
    summed = jnp.sum(received.astype(jnp.float32), axis=0)
    return summed / dp_count


def body(
    expand_gradient,
    expand_master,
    expand_rows,
    expand_columns,
    contract_gradient,
    contract_master,
    contract_rows,
    contract_columns,
    attend_gradient,
    attend_master,
    attend_rows,
    attend_columns,
):
    groups = (
        (expand_gradient, expand_master, expand_rows, expand_columns),
        (contract_gradient, contract_master, contract_rows, contract_columns),
        (attend_gradient, attend_master, attend_rows, attend_columns),
    )
    dp_count = lax.axis_size("dp")
    col_count = lax.axis_size("col")
    split_count = dp_count * lax.axis_size(ROW)
    means = []
    for gradient, master, row_stat, column_stat in groups:
        means.append(reduce_gradient(gradient, dp_count))
    squares = [mean_grad * mean_grad + tiny_square for mean_grad in means]
    row_parts = [jnp.sum(square_block, axis=1) for square_block in squares]
    column_parts = [jnp.sum(square_block, axis=0) for square_block in squares]
    heights = [mean_grad.shape[0] * split_count for mean_grad in means]
    widths = [mean_grad.shape[1] * col_count for mean_grad in means]
    outputs = []
    row_totals = packed_total((row_parts[0], row_parts[1], row_parts[2]), "col")
    rows_next = [
        decay_rate * groups[which][2] + (1.0 - decay_rate) * row_totals[which] / widths[which]
        for which in range(3)
    ]
    joined = (
        one_axis_at_a_time(column_parts[0], DP_ROW),
        one_axis_at_a_time(column_parts[1], DP_ROW),
        one_axis_at_a_time(column_parts[2], DP_ROW),
        one_axis_at_a_time(jnp.sum(rows_next[0]), DP_ROW),
        one_axis_at_a_time(jnp.sum(rows_next[1]), DP_ROW),
        one_axis_at_a_time(jnp.sum(rows_next[2]), DP_ROW),
    )
    columns_next = [
        decay_rate * groups[which][3] + (1.0 - decay_rate) * joined[which] / heights[which]
        for which in range(3)
    ]
    raws = [
        means[which]
        * jnp.sqrt(
            joined[3 + which]
            / heights[which]
            / (rows_next[which][:, None] * columns_next[which][None, :])
        )
        for which in range(3)
    ]
    clips = (
        one_axis_at_a_time(jnp.sum(raws[0] * raws[0]), DP_ROW_COL),
        one_axis_at_a_time(jnp.sum(raws[1] * raws[1]), DP_ROW_COL),
        one_axis_at_a_time(jnp.sum(raws[2] * raws[2]), DP_ROW_COL),
    )
    for which in range(3):
        updated, weights, step_taken = finish(
            raws[which], clips[which], groups[which][1], heights[which] * widths[which]
        )
        outputs.extend([updated, weights, rows_next[which], columns_next[which], step_taken])
    return tuple(outputs)


def solution(mesh):
    finer = Mesh(
        mesh.devices.reshape(mesh.shape["dp"], 2, 4, 2, mesh.shape["col"]),
        ("dp", "row_0", "row_1", "row_2", "col"),
    )
    in_specs = (
        P("dp", ROW, "col"),
        P(ROW_DP, "col"),
        P(ROW_DP),
        P("col"),
        P("dp", ROW, "col"),
        P(ROW_DP, "col"),
        P(ROW_DP),
        P("col"),
        P("dp", ROW, "col"),
        P(ROW_DP, "col"),
        P(ROW_DP),
        P("col"),
    )
    out_specs = (
        P(ROW_DP, "col"),
        P(ROW, "col"),
        P(ROW_DP),
        P("col"),
        P(ROW_DP, "col"),
        P(ROW_DP, "col"),
        P(ROW, "col"),
        P(ROW_DP),
        P("col"),
        P(ROW_DP, "col"),
        P(ROW_DP, "col"),
        P(ROW, "col"),
        P(ROW_DP),
        P("col"),
        P(ROW_DP, "col"),
    )
    return jax.shard_map(body, mesh=finer, in_specs=in_specs, out_specs=out_specs, check_vma=False)
```

profile of v0, /device:TPU:2, one launch (start us, length us, event | category | flops | bytes accessed | tf_op | source)
XLA Modules:
  0.0 415.7 jit_solution(8251407359261963405)
XLA Ops:
  3.0 3.7 reduce.2
  7.9 12.5 %all-to-all-start.2 = ((bf16[8,2,16384]{2,1,0:T(2,128)(2,1)}), bf16[8,2,16384]{2,1,0:T(2,128)(2,1)S(1)}, u32[]{:S(2)}, u32[]{:S(2)}) async-start(bf16[8,2,16384]{2,1,0:T(2,128)(2,1)} %reshape.72), calls=%async_computation.2 | async-start | bytes 1048576 | tf_op jit(solution)/shard_map/all_to_all | solution.py:59
  21.4 4.6 %reduce.1 = bf16[256,1280]{1,0:T(8,128)(2,1)S(1)} reduce(bf16[256,1,1280]{2,1,0:T(2,128)(2,1)S(1)} %bitcast.23, bf16[]{:T(256)} %broadcast.40), dimensions={1}, to_apply=%bitcast.20.reduce_sub_computation | reduce | bytes 1310722
  27.1 22.1 %all-to-all-done.2 = bf16[8,2,16384]{2,1,0:T(2,128)(2,1)S(1)} async-done(((bf16[8,2,16384]{2,1,0:T(2,128)(2,1)}), bf16[8,2,16384]{2,1,0:T(2,128)(2,1)S(1)}, u32[]{:S(2)}, u32[]{:S(2)}) %all-to-all-start.2) | async-done | bytes 524320 | tf_op jit(solution)/shard_map/all_to_all | solution.py:59
  49.9 4.3 %all-to-all-start = ((bf16[8,2,20480]{2,1,0:T(2,128)(2,1)}), bf16[8,2,20480]{2,1,0:T(2,128)(2,1)S(1)}, u32[]{:S(2)}, u32[]{:S(2)}) async-start(bf16[8,2,20480]{2,1,0:T(2,128)(2,1)} %reshape.70), calls=%async_computation | async-start | bytes 1310720 | tf_op jit(solution)/shard_map/all_to_all | solution.py:59
  55.2 4.5 %reduce.3 = bf16[320,1024]{1,0:T(8,128)(2,1)S(1)} reduce(bf16[320,1,1024]{2,1,0:T(2,128)(2,1)S(1)} %bitcast.22, bf16[]{:T(256)} %broadcast.40), dimensions={1}, to_apply=%bitcast.19.reduce_sub_computation | reduce | bytes 1310722
  61.0 27.3 %all-to-all-done = bf16[8,2,20480]{2,1,0:T(2,128)(2,1)S(1)} async-done(((bf16[8,2,20480]{2,1,0:T(2,128)(2,1)}), bf16[8,2,20480]{2,1,0:T(2,128)(2,1)S(1)}, u32[]{:S(2)}, u32[]{:S(2)}) %all-to-all-start) | async-done | bytes 655392 | tf_op jit(solution)/shard_map/all_to_all | solution.py:59
  88.2 4.3 %all-to-all-start.1 = ((bf16[8,2,20480]{2,1,0:T(2,128)(2,1)}), bf16[8,2,20480]{2,1,0:T(2,128)(2,1)S(1)}, u32[]{:S(2)}, u32[]{:S(2)}) async-start(bf16[8,2,20480]{2,1,0:T(2,128)(2,1)} %reshape.74), calls=%async_computation.1 | async-start | bytes 1310720 | tf_op jit(solution)/shard_map/all_to_all | solution.py:59
  94.4 31.9 %all-to-all-done.1 = bf16[8,2,20480]{2,1,0:T(2,128)(2,1)S(1)} async-done(((bf16[8,2,20480]{2,1,0:T(2,128)(2,1)}), bf16[8,2,20480]{2,1,0:T(2,128)(2,1)S(1)}, u32[]{:S(2)}, u32[]{:S(2)}) %all-to-all-start.1) | async-done | bytes 655392 | tf_op jit(solution)/shard_map/all_to_all | solution.py:59
  127.7 9.5 %all_to_all.48 = f32[4,1,104]{2,1,0:T(1,128)S(1)} all-to-all(f32[4,1,104]{2,1,0:T(1,128)S(1)} %broadcast_in_dim.8), channel_id=1, replica_groups=mesh['dp'=8,'row_0'=2,'row_1'=4,'row_2'=2,'col'=4] {'col'}, dimensions={0} | all-to-all | bytes 3328 | tf_op jit(solution)/shard_map/all_to_all | solution.py:24
  138.6 52.8 %all-reduce.1 = (f32[1280]{0:T(1024)S(1)}, f32[]{:T(128)}, f32[1024]{0:T(1024)S(1)}, f32[]{:T(128)}, f32[1024]{0:T(1024)S(1)}, /*index=5*/f32[]{:T(128)}) all-reduce(f32[1280]{0:T(1024)S(1)} %get-tuple-element.18, f32[]{:T(128)} %get-tuple-element.75, ...), channel_id=1, replica_groups=mesh['dp'=8,'row_0'=2,'row_1'=4,'row_2'=2,'col'=4] {'dp'}, use_global_device_ids=true, to_apply=%region_13.0 | all-reduce | flops 3331 | bytes 26648 | tf_op jit(solution)/shard_map/psum | solution.py:46
  191.4 23.0 %all-reduce.8 = (f32[1280]{0:T(1024)S(1)}, f32[]{:T(128)}, f32[1024]{0:T(1024)S(1)}, f32[]{:T(128)}, f32[1024]{0:T(1024)S(1)}, /*index=5*/f32[]{:T(128)}) all-reduce(f32[1280]{0:T(1024)S(1)} %get-tuple-element.24, f32[]{:T(128)} %get-tuple-element.25, ...), channel_id=1, replica_groups=mesh['dp'=8,'row_0'=2,'row_1'=4,'row_2'=2,'col'=4] {'row_0'}, use_global_device_ids=true, to_apply=%region_14.0 | all-reduce | flops 3331 | bytes 26648 | tf_op jit(solution)/shard_map/psum | solution.py:46
  214.4 15.2 %all-reduce.4 = (f32[1280]{0:T(1024)S(1)}, f32[]{:T(128)}, f32[1024]{0:T(1024)S(1)}, f32[]{:T(128)}, f32[1024]{0:T(1024)S(1)}, /*index=5*/f32[]{:T(128)}) all-reduce(f32[1280]{0:T(1024)S(1)} %get-tuple-element.54, f32[]{:T(128)} %get-tuple-element.55, ...), channel_id=1, replica_groups=mesh['dp'=8,'row_0'=2,'row_1'=4,'row_2'=2,'col'=4] {'row_1'}, use_global_device_ids=true, to_apply=%region_15.0 | all-reduce | flops 3331 | bytes 26648 | tf_op jit(solution)/shard_map/psum | solution.py:46
  229.6 4.5 %all-reduce.6 = (f32[1280]{0:T(1024)S(1)}, f32[]{:T(128)}, f32[1024]{0:T(1024)S(1)}, f32[]{:T(128)}, f32[1024]{0:T(1024)S(1)}, /*index=5*/f32[]{:T(128)}) all-reduce(f32[1280]{0:T(1024)S(1)} %get-tuple-element.36, f32[]{:T(128)} %get-tuple-element.37, ...), channel_id=1, replica_groups=mesh['dp'=8,'row_0'=2,'row_1'=4,'row_2'=2,'col'=4] {'row_2'}, use_global_device_ids=true, to_apply=%region_16.0 | all-reduce | flops 3331 | bytes 26648 | tf_op jit(solution)/shard_map/psum | solution.py:46
  238.3 25.7 %all-reduce = (f32[]{:T(128)}, f32[]{:T(128)}, f32[]{:T(128)}) all-reduce(f32[]{:T(128)} %multiply_reduce_fusion.1, f32[]{:T(128)} %multiply_reduce_fusion, f32[]{:T(128)} %multiply_reduce_fusion.2), channel_id=1, replica_groups=mesh['dp'=8,'row_0'=2,'row_1'=4,'row_2'=2,'col'=4] {'dp'}, use_global_device_ids=true, to_apply=%region_18.0 | all-reduce | flops 3 | bytes 24 | tf_op jit(solution)/shard_map/psum | solution.py:46
  264.0 14.3 %all-reduce.7 = (f32[]{:T(128)}, f32[]{:T(128)}, f32[]{:T(128)}) all-reduce(f32[]{:T(128)} %get-tuple-element.21, f32[]{:T(128)} %get-tuple-element.22, f32[]{:T(128)} %get-tuple-element.23), channel_id=1, replica_groups=mesh['dp'=8,'row_0'=2,'row_1'=4,'row_2'=2,'col'=4] {'row_0'}, use_global_device_ids=true, to_apply=%region_19.0 | all-reduce | flops 3 | bytes 24 | tf_op jit(solution)/shard_map/psum | solution.py:46
  278.2 11.8 %all-reduce.3 = (f32[]{:T(128)}, f32[]{:T(128)}, f32[]{:T(128)}) all-reduce(f32[]{:T(128)} %get-tuple-element.51, f32[]{:T(128)} %get-tuple-element.52, f32[]{:T(128)} %get-tuple-element.53), channel_id=1, replica_groups=mesh['dp'=8,'row_0'=2,'row_1'=4,'row_2'=2,'col'=4] {'row_1'}, use_global_device_ids=true, to_apply=%region_20.0 | all-reduce | flops 3 | bytes 24 | tf_op jit(solution)/shard_map/psum | solution.py:46
  293.2 9.5 %all-reduce.2 = (f32[]{:T(128)}, f32[]{:T(128)}, f32[]{:T(128)}) all-reduce(f32[]{:T(128)} %get-tuple-element.42, f32[]{:T(128)} %get-tuple-element.43, f32[]{:T(128)} %get-tuple-element.44), channel_id=1, replica_groups=mesh['dp'=8,'row_0'=2,'row_1'=4,'row_2'=2,'col'=4] {'col'}, use_global_device_ids=true, to_apply=%region_22.0 | all-reduce | flops 3 | bytes 24 | tf_op jit(solution)/shard_map/psum | solution.py:46
  305.1 3.5 all-to-all-start.6
  310.2 25.6 %all-to-all-done.6 = bf16[8,32,1024]{2,1,0:T(8,128)(2,1)S(1)} async-done(((bf16[8,32,1024]{2,1,0:T(8,128)(2,1)}), bf16[8,32,1024]{2,1,0:T(8,128)(2,1)S(1)}, u32[]{:S(2)}, u32[]{:S(2)}) %all-to-all-start.6) | async-done | bytes 524320 | tf_op jit(solution)/shard_map/all_to_all | solution.py:24
  336.7 4.3 %all-to-all-start.4 = ((bf16[8,32,1280]{2,1,0:T(8,128)(2,1)}), bf16[8,32,1280]{2,1,0:T(8,128)(2,1)S(1)}, u32[]{:S(2)}, u32[]{:S(2)}) async-start(bf16[8,32,1280]{2,1,0:T(8,128)(2,1)} %broadcast_in_dim.9), calls=%async_computation.4 | async-start | bytes 1310720 | tf_op jit(solution)/shard_map/all_to_all | solution.py:24
  342.6 32.0 %all-to-all-done.4 = bf16[8,32,1280]{2,1,0:T(8,128)(2,1)S(1)} async-done(((bf16[8,32,1280]{2,1,0:T(8,128)(2,1)}), bf16[8,32,1280]{2,1,0:T(8,128)(2,1)S(1)}, u32[]{:S(2)}, u32[]{:S(2)}) %all-to-all-start.4) | async-done | bytes 655392 | tf_op jit(solution)/shard_map/all_to_all | solution.py:24
  375.5 4.3 %all-to-all-start.5 = ((bf16[8,40,1024]{2,1,0:T(8,128)(2,1)}), bf16[8,40,1024]{2,1,0:T(8,128)(2,1)S(1)}, u32[]{:S(2)}, u32[]{:S(2)}) async-start(bf16[8,40,1024]{2,1,0:T(8,128)(2,1)} %broadcast_in_dim.20), calls=%async_computation.5 | async-start | bytes 1310720 | tf_op jit(solution)/shard_map/all_to_all | solution.py:24
  379.8 33.5 %all-to-all-done.5 = bf16[8,40,1024]{2,1,0:T(8,128)(2,1)S(1)} async-done(((bf16[8,40,1024]{2,1,0:T(8,128)(2,1)}), bf16[8,40,1024]{2,1,0:T(8,128)(2,1)S(1)}, u32[]{:S(2)}, u32[]{:S(2)}) %all-to-all-start.5) | async-done | bytes 655392 | tf_op jit(solution)/shard_map/all_to_all | solution.py:24
  (77 shorter events, 26.2 us)
Async XLA Ops:
  6.7 13.7 %copy-start.2 = (bf16[1,256,1280]{2,1,0:T(8,128)(2,1)S(1)}, bf16[1,256,1280]{2,1,0:T(8,128)(2,1)}, u32[]{:S(2)}) copy-start(bf16[1,256,1280]{2,1,0:T(8,128)(2,1)} %param.12) | copy-start | bytes 1966084
  7.9 41.3 %all-to-all-start.2 = ((bf16[8,2,16384]{2,1,0:T(2,128)(2,1)}), bf16[8,2,16384]{2,1,0:T(2,128)(2,1)S(1)}, u32[]{:S(2)}, u32[]{:S(2)}) async-start(bf16[8,2,16384]{2,1,0:T(2,128)(2,1)} %reshape.72), calls=%async_computation.2 | async-start | bytes 1048576 | tf_op jit(solution)/shard_map/all_to_all | solution.py:59
  26.1 28.1 %copy-start.3 = (bf16[1,320,1024]{2,1,0:T(8,128)(2,1)S(1)}, bf16[1,320,1024]{2,1,0:T(8,128)(2,1)}, u32[]{:S(2)}) copy-start(bf16[1,320,1024]{2,1,0:T(8,128)(2,1)} %param.16) | copy-start | bytes 1966084
  49.9 38.3 %all-to-all-start = ((bf16[8,2,20480]{2,1,0:T(2,128)(2,1)}), bf16[8,2,20480]{2,1,0:T(2,128)(2,1)S(1)}, u32[]{:S(2)}, u32[]{:S(2)}) async-start(bf16[8,2,20480]{2,1,0:T(2,128)(2,1)} %reshape.70), calls=%async_computation | async-start | bytes 1310720 | tf_op jit(solution)/shard_map/all_to_all | solution.py:59
  61.0 31.6 %copy-start.1 = (bf16[8,2,16384]{2,1,0:T(2,128)(2,1)S(1)}, bf16[8,2,16384]{2,1,0:T(2,128)(2,1)}, u32[]{:S(2)}) copy-start(bf16[8,2,16384]{2,1,0:T(2,128)(2,1)} %copy-done) | copy-start | bytes 1572868
  88.2 38.2 %all-to-all-start.1 = ((bf16[8,2,20480]{2,1,0:T(2,128)(2,1)}), bf16[8,2,20480]{2,1,0:T(2,128)(2,1)S(1)}, u32[]{:S(2)}, u32[]{:S(2)}) async-start(bf16[8,2,20480]{2,1,0:T(2,128)(2,1)} %reshape.74), calls=%async_computation.1 | async-start | bytes 1310720 | tf_op jit(solution)/shard_map/all_to_all | solution.py:59
  127.0 10.2 %copy-start.16 = (f32[40]{0:T(128)S(1)}, f32[40]{0:T(128)}, u32[]{:S(2)}) copy-start(f32[40]{0:T(128)} %param.18) | copy-start | bytes 484
  127.0 10.9 %copy-start.17 = (f32[32]{0:T(128)S(1)}, f32[32]{0:T(128)}, u32[]{:S(2)}) copy-start(f32[32]{0:T(128)} %param.22) | copy-start | bytes 388
  127.0 10.8 %copy-start.18 = (f32[32]{0:T(128)S(1)}, f32[32]{0:T(128)}, u32[]{:S(2)}) copy-start(f32[32]{0:T(128)} %param.14) | copy-start | bytes 388
  127.1 108.3 %copy-start.10 = (f32[1280]{0:T(1024)S(1)}, f32[1280]{0:T(1024)}, u32[]{:S(2)}) copy-start(f32[1280]{0:T(1024)} %param.15) | copy-start | bytes 15364
  127.1 109.7 %copy-start.14 = (f32[1024]{0:T(1024)S(1)}, f32[1024]{0:T(1024)}, u32[]{:S(2)}) copy-start(f32[1024]{0:T(1024)} %param.23) | copy-start | bytes 12292
  127.1 109.7 %copy-start.15 = (f32[1024]{0:T(1024)S(1)}, f32[1024]{0:T(1024)}, u32[]{:S(2)}) copy-start(f32[1024]{0:T(1024)} %param.19) | copy-start | bytes 12292
  127.3 176.0 %copy-start.6 = (f32[32,1024]{1,0:T(8,128)S(1)}, f32[32,1024]{1,0:T(8,128)}, u32[]{:S(2)}) copy-start(f32[32,1024]{1,0:T(8,128)} %param.21) | copy-start | bytes 393220
  137.9 203.8 %copy-start.11 = (f32[40]{0:T(128)}, f32[40]{0:T(128)S(1)}, u32[]{:S(2)}) copy-start(f32[40]{0:T(128)S(1)} %get-tuple-element.101) | copy-start | bytes 484
  138.6 166.5 %copy-start.13 = (f32[32]{0:T(128)}, f32[32]{0:T(128)S(1)}, u32[]{:S(2)}) copy-start(f32[32]{0:T(128)S(1)} %get-tuple-element.106) | copy-start | bytes 388
  138.6 170.7 %copy-start.12 = (f32[32]{0:T(128)}, f32[32]{0:T(128)S(1)}, u32[]{:S(2)}) copy-start(f32[32]{0:T(128)S(1)} %get-tuple-element.96) | copy-start | bytes 388
  235.4 73.9 %copy-start.7 = (f32[1280]{0:T(1024)}, f32[1280]{0:T(1024)S(1)}, u32[]{:S(2)}) copy-start(f32[1280]{0:T(1024)S(1)} %multiply_add_fusion.3) | copy-start | bytes 15364
  236.8 72.5 %copy-start.4 = (f32[32,1280]{1,0:T(8,128)S(1)}, f32[32,1280]{1,0:T(8,128)}, u32[]{:S(2)}) copy-start(f32[32,1280]{1,0:T(8,128)} %param.13) | copy-start | bytes 491524
  236.8 73.4 %copy-start.8 = (f32[1024]{0:T(1024)}, f32[1024]{0:T(1024)S(1)}, u32[]{:S(2)}) copy-start(f32[1024]{0:T(1024)S(1)} %get-tuple-element.107) | copy-start | bytes 12292
  236.8 104.9 %copy-start.9 = (f32[1024]{0:T(1024)}, f32[1024]{0:T(1024)S(1)}, u32[]{:S(2)}) copy-start(f32[1024]{0:T(1024)S(1)} %get-tuple-element.102) | copy-start | bytes 12292
  305.1 30.7 %all-to-all-start.6 = ((bf16[8,32,1024]{2,1,0:T(8,128)(2,1)}), bf16[8,32,1024]{2,1,0:T(8,128)(2,1)S(1)}, u32[]{:S(2)}, u32[]{:S(2)}) async-start(bf16[8,32,1024]{2,1,0:T(8,128)(2,1)} %broadcast_in_dim.21), calls=%async_computation.6 | async-start | bytes 1048576 | tf_op jit(solution)/shard_map/all_to_all | solution.py:24
  309.3 32.4 %copy-start.5 = (f32[40,1024]{1,0:T(8,128)S(1)}, f32[40,1024]{1,0:T(8,128)}, u32[]{:S(2)}) copy-start(f32[40,1024]{1,0:T(8,128)} %param.17) | copy-start | bytes 491524
  336.7 37.9 %all-to-all-start.4 = ((bf16[8,32,1280]{2,1,0:T(8,128)(2,1)}), bf16[8,32,1280]{2,1,0:T(8,128)(2,1)S(1)}, u32[]{:S(2)}, u32[]{:S(2)}) async-start(bf16[8,32,1280]{2,1,0:T(8,128)(2,1)} %broadcast_in_dim.9), calls=%async_computation.4 | async-start | bytes 1310720 | tf_op jit(solution)/shard_map/all_to_all | solution.py:24
  375.5 37.8 %all-to-all-start.5 = ((bf16[8,40,1024]{2,1,0:T(8,128)(2,1)}), bf16[8,40,1024]{2,1,0:T(8,128)(2,1)S(1)}, u32[]{:S(2)}, u32[]{:S(2)}) async-start(bf16[8,40,1024]{2,1,0:T(8,128)(2,1)} %broadcast_in_dim.20), calls=%async_computation.5 | async-start | bytes 1310720 | tf_op jit(solution)/shard_map/all_to_all | solution.py:24
  (1 other events, 0.8 us)
where the time goes:
time: 417 us; the launch traced here: 416 us
  waiting for transfers between devices  172 us (41%)
  blocking collectives  169 us (41%)
  starting transfers between devices  33.2 us (8%)
  other arithmetic  19.8 us (5%)
  local copies, waits for them, and re-layouts  16.1 us (4%)
  between operations  5 us (1%)
    psum x9, blocking collectives, one_axis_at_a_time(): shard = lax.psum(shard, axis)  160 us
    all_to_all x3, waiting for transfers between devices, from_everyone(): return lax.all_to_all(copies, axis, split_axis=0, concat_axis=0, tiled=True)  91.1 us
    all_to_all x3, waiting for transfers between devices, reduce_gradient(): lax.all_to_all(gradient, 'dp', split_axis=1, concat_axis=0, tiled=True)  81.3 us
    all_to_all x3, starting transfers between devices, reduce_gradient(): lax.all_to_all(gradient, 'dp', split_axis=1, concat_axis=0, tiled=True)  21.1 us
    unnamed x51, local copies, waits for them, and re-layouts  13 us
    unnamed x3, other arithmetic  12.8 us
    all_to_all x3, starting transfers between devices, from_everyone(): return lax.all_to_all(copies, axis, split_axis=0, concat_axis=0, tiled=True)  12.1 us
    all_to_all x1, blocking collectives, from_everyone(): return lax.all_to_all(copies, axis, split_axis=0, concat_axis=0, tiled=True)  9.54 us
  transfers between devices with their start and end apart: 6, of which 6 were waited for; matrix products, arithmetic and copies ran while one was open for 4% of the time, Pallas kernels for 0%

commit v1 on v0

--- a/solution.py
+++ b/solution.py
@@ -11,6 +11,12 @@
 tiny_square = 1e-30
 decay_rate = 0.9
 learn_rate = 0.01
+
+
+def add_all(block, axis):
+    pieces = lax.all_gather(block, axis, axis=0, tiled=False)
+    summed = pieces.sum(axis=0)
+    return summed
 
 
 def in_order(blocks, dim):
@@ -43,7 +49,7 @@
 
 def one_axis_at_a_time(shard, axes):
     for axis in axes:
-        shard = lax.psum(shard, axis)
+        shard = add_all(shard, axis)
     return shard
 
 

time: 417 us -> 622 us (1.49)
  blocking collectives: 169 us -> 342 us
  local copies, waits for them, and re-layouts: 16.1 us -> 60.3 us
  waiting for transfers between devices: 172 us -> 139 us
  other arithmetic: 19.8 us -> 36.2 us
    all_gather x0 -> x12, blocking collectives: none -> 224 us  [add_all(): pieces = lax.all_gather(block, axis, axis=0, tiled=False)]
    psum x9 -> x0, blocking collectives: 160 us -> none  [one_axis_at_a_time(): shard = lax.psum(shard, axis)]
    unnamed x0 -> x9, blocking collectives: none -> 117 us
    unnamed x51 -> x110, local copies, waits for them, and re-layouts: 13 us -> 56.6 us
    all_to_all x3, waiting for transfers between devices: 81.3 us -> 49.4 us  [reduce_gradient(): lax.all_to_all(gradient, 'dp', split_axis=1, concat_axis=0, tiled=True)]
    reduce_sum x0 -> x39, other arithmetic: none -> 16.5 us  [add_all(): summed = pieces.sum(axis=0)]
    all_to_all x1 -> x0, blocking collectives: 9.54 us -> none  [from_everyone(): return lax.all_to_all(copies, axis, split_axis=0, concat_axis=0, tiled=True)]
    all_to_all x3 -> x4, starting transfers between devices: 12.1 us -> 16.5 us  [from_everyone(): return lax.all_to_all(copies, axis, split_axis=0, concat_axis=0, tiled=True)]
  transfers between devices with their start and end apart: 6 -> 7, of which waited for: 6 -> 5; matrix products, arithmetic and copies ran while one was open for 4% -> 4% of each run, Pallas kernels for 0% -> 0%
where the time goes in v1:
time: 622 us; the launch traced here: 620 us
  blocking collectives  342 us (55%)
  waiting for transfers between devices  139 us (22%)
  local copies, waits for them, and re-layouts  60.3 us (10%)
  starting transfers between devices  37.6 us (6%)
  other arithmetic  36.2 us (6%)
    all_gather x12, blocking collectives, add_all(): pieces = lax.all_gather(block, axis, axis=0, tiled=False)  224 us
    unnamed x9, blocking collectives  117 us
    all_to_all x4, waiting for transfers between devices, from_everyone(): return lax.all_to_all(copies, axis, split_axis=0, concat_axis=0, tiled=True)  89.9 us
    unnamed x110, local copies, waits for them, and re-layouts  56.6 us
    all_to_all x3, waiting for transfers between devices, reduce_gradient(): lax.all_to_all(gradient, 'dp', split_axis=1, concat_axis=0, tiled=True)  49.4 us
    all_to_all x3, starting transfers between devices, reduce_gradient(): lax.all_to_all(gradient, 'dp', split_axis=1, concat_axis=0, tiled=True)  21.1 us
    all_to_all x4, starting transfers between devices, from_everyone(): return lax.all_to_all(copies, axis, split_axis=0, concat_axis=0, tiled=True)  16.5 us
    reduce_sum x39, other arithmetic, add_all(): summed = pieces.sum(axis=0)  16.5 us
  transfers between devices with their start and end apart: 7, of which 5 were waited for; matrix products, arithmetic and copies ran while one was open for 4% of the time, Pallas kernels for 0%

profile of v1, /device:TPU:2, one launch (start us, length us, event | category | flops | bytes accessed | tf_op | source)
XLA Modules:
  0.0 620.4 jit_solution(1741721965191888897)
XLA Ops:
  7.9 12.5 %all-to-all-start.2 = ((bf16[8,2,16384]{2,1,0:T(2,128)(2,1)}), bf16[8,2,16384]{2,1,0:T(2,128)(2,1)S(1)}, u32[]{:S(2)}, u32[]{:S(2)}) async-start(bf16[8,2,16384]{2,1,0:T(2,128)(2,1)} %reshape.231), calls=%async_computation.2 | async-start | bytes 1048576 | tf_op jit(solution)/shard_map/all_to_all | solution.py:65
  21.4 4.6 reduce.32
  27.1 22.1 %all-to-all-done.2 = bf16[8,2,16384]{2,1,0:T(2,128)(2,1)S(1)} async-done(((bf16[8,2,16384]{2,1,0:T(2,128)(2,1)}), bf16[8,2,16384]{2,1,0:T(2,128)(2,1)S(1)}, u32[]{:S(2)}, u32[]{:S(2)}) %all-to-all-start.2) | async-done | bytes 524320 | tf_op jit(solution)/shard_map/all_to_all | solution.py:65
  54.4 4.5 reduce.34
  60.2 27.3 %all-to-all-done = bf16[8,2,20480]{2,1,0:T(2,128)(2,1)S(1)} async-done(((bf16[8,2,20480]{2,1,0:T(2,128)(2,1)}), bf16[8,2,20480]{2,1,0:T(2,128)(2,1)S(1)}, u32[]{:S(2)}, u32[]{:S(2)}) %all-to-all-start) | async-done | bytes 655392 | tf_op jit(solution)/shard_map/all_to_all | solution.py:65
  97.7 50.9 %all-gather.8 = f32[8192]{0:T(1024)S(1)} all-gather(f32[1024]{0:T(1024)S(1)} %get-tuple-element.19), channel_id=10, replica_groups=mesh['dp'=8,'row_0'=2,'row_1'=4,'row_2'=2,'col'=4] {'dp'}, dimensions={0}, use_global_device_ids=true | all-gather | bytes 36864 | tf_op jit(solution)/shard_map/all_gather | solution.py:17
  148.7 13.1 %all-gather.9 = f32[2048]{0:T(1024)S(1)} all-gather(f32[1024]{0:T(1024)S(1)} %reduce_sum.540), channel_id=11, replica_groups=mesh['dp'=8,'row_0'=2,'row_1'=4,'row_2'=2,'col'=4] {'row_0'}, dimensions={0}, use_global_device_ids=true | all-gather | bytes 12288 | tf_op jit(solution)/shard_map/all_gather | solution.py:17
  161.8 12.1 %all-gather.10 = f32[4096]{0:T(1024)S(1)} all-gather(f32[1024]{0:T(1024)S(1)} %reduce_sum.541), channel_id=12, replica_groups=mesh['dp'=8,'row_0'=2,'row_1'=4,'row_2'=2,'col'=4] {'row_1'}, dimensions={0}, use_global_device_ids=true | all-gather | bytes 20480 | tf_op jit(solution)/shard_map/all_gather | solution.py:17
  176.7 46.4 %all-gather.12 = f32[8,1,1280]{2,1,0:T(1,128)S(1)} all-gather(f32[1,1,1280]{2,1,0:T(1,128)S(1)} %reshape.163), channel_id=2, replica_groups=mesh['dp'=8,'row_0'=2,'row_1'=4,'row_2'=2,'col'=4] {'dp'}, dimensions={0}, use_global_device_ids=true | all-gather | bytes 46080 | tf_op jit(solution)/shard_map/all_gather | solution.py:17
  223.1 13.1 %all-gather.13 = f32[2,1,1280]{2,1,0:T(1,128)S(1)} all-gather(f32[1,1,1280]{2,1,0:T(1,128)S(1)} %reshape.165), channel_id=3, replica_groups=mesh['dp'=8,'row_0'=2,'row_1'=4,'row_2'=2,'col'=4] {'row_0'}, dimensions={0}, use_global_device_ids=true | all-gather | bytes 15360 | tf_op jit(solution)/shard_map/all_gather | solution.py:17
  236.3 12.0 %all-gather.14 = f32[4,1,1280]{2,1,0:T(1,128)S(1)} all-gather(f32[1,1,1280]{2,1,0:T(1,128)S(1)} %reshape.167), channel_id=4, replica_groups=mesh['dp'=8,'row_0'=2,'row_1'=4,'row_2'=2,'col'=4] {'row_1'}, dimensions={0}, use_global_device_ids=true | all-gather | bytes 25600 | tf_op jit(solution)/shard_map/all_gather | solution.py:17
  256.5 46.3 %all-gather.4 = f32[8192]{0:T(1024)S(1)} all-gather(f32[1024]{0:T(1024)S(1)} %get-tuple-element.15), channel_id=6, replica_groups=mesh['dp'=8,'row_0'=2,'row_1'=4,'row_2'=2,'col'=4] {'dp'}, dimensions={0}, use_global_device_ids=true | all-gather | bytes 36864 | tf_op jit(solution)/shard_map/all_gather | solution.py:17
  302.8 13.1 %all-gather.5 = f32[2048]{0:T(1024)S(1)} all-gather(f32[1024]{0:T(1024)S(1)} %reduce_sum.524), channel_id=7, replica_groups=mesh['dp'=8,'row_0'=2,'row_1'=4,'row_2'=2,'col'=4] {'row_0'}, dimensions={0}, use_global_device_ids=true | all-gather | bytes 12288 | tf_op jit(solution)/shard_map/all_gather | solution.py:17
  315.9 12.0 %all-gather.6 = f32[4096]{0:T(1024)S(1)} all-gather(f32[1024]{0:T(1024)S(1)} %reduce_sum.525), channel_id=8, replica_groups=mesh['dp'=8,'row_0'=2,'row_1'=4,'row_2'=2,'col'=4] {'row_1'}, dimensions={0}, use_global_device_ids=true | all-gather | bytes 20480 | tf_op jit(solution)/shard_map/all_gather | solution.py:17
  335.4 30.6 %all-reduce.28 = (f32[8]{0:T(128)S(1)}, f32[8]{0:T(128)S(1)}, f32[8]{0:T(128)S(1)}) all-reduce(f32[8]{0:T(128)S(1)} %dynamic-update-slice, f32[8]{0:T(128)S(1)} %dynamic-update-slice.9, f32[8]{0:T(128)S(1)} %dynamic-update-slice.18), channel_id=1, replica_groups=mesh['dp'=8,'row_0'=2,'row_1'=4,'row_2'=2,'col'=4] {'dp'}, use_global_device_ids=true, to_apply=%add | all-reduce | flops 24 | bytes 192
  372.1 13.6 %all-reduce.35 = (f32[2]{0:T(128)S(1)}, f32[2]{0:T(128)S(1)}, f32[2]{0:T(128)S(1)}) all-reduce(f32[2]{0:T(128)S(1)} %dynamic-update-slice.1, f32[2]{0:T(128)S(1)} %dynamic-update-slice.10, f32[2]{0:T(128)S(1)} %dynamic-update-slice.19), channel_id=1, replica_groups=mesh['dp'=8,'row_0'=2,'row_1'=4,'row_2'=2,'col'=4] {'row_0'}, use_global_device_ids=true, to_apply=%add.1 | all-reduce | flops 6 | bytes 48
  391.8 8.6 %all-reduce.31 = (f32[4]{0:T(128)S(1)}, f32[4]{0:T(128)S(1)}, f32[4]{0:T(128)S(1)}) all-reduce(f32[4]{0:T(128)S(1)} %dynamic-update-slice.2, f32[4]{0:T(128)S(1)} %dynamic-update-slice.11, f32[4]{0:T(128)S(1)} %dynamic-update-slice.20), channel_id=1, replica_groups=mesh['dp'=8,'row_0'=2,'row_1'=4,'row_2'=2,'col'=4] {'row_1'}, use_global_device_ids=true, to_apply=%add.2 | all-reduce | flops 12 | bytes 96
  419.2 25.0 %all-reduce.27 = (f32[8]{0:T(128)S(1)}, f32[8]{0:T(128)S(1)}, f32[8]{0:T(128)S(1)}) all-reduce(f32[8]{0:T(128)S(1)} %dynamic-update-slice.4, f32[8]{0:T(128)S(1)} %dynamic-update-slice.13, f32[8]{0:T(128)S(1)} %dynamic-update-slice.22), channel_id=1, replica_groups=mesh['dp'=8,'row_0'=2,'row_1'=4,'row_2'=2,'col'=4] {'dp'}, use_global_device_ids=true, to_apply=%add.4 | all-reduce | flops 24 | bytes 192
  450.3 13.6 %all-reduce.34 = (f32[2]{0:T(128)S(1)}, f32[2]{0:T(128)S(1)}, f32[2]{0:T(128)S(1)}) all-reduce(f32[2]{0:T(128)S(1)} %dynamic-update-slice.5, f32[2]{0:T(128)S(1)} %dynamic-update-slice.14, f32[2]{0:T(128)S(1)} %dynamic-update-slice.23), channel_id=1, replica_groups=mesh['dp'=8,'row_0'=2,'row_1'=4,'row_2'=2,'col'=4] {'row_0'}, use_global_device_ids=true, to_apply=%add.5 | all-reduce | flops 6 | bytes 48
  469.9 10.1 %all-reduce.30 = (f32[4]{0:T(128)S(1)}, f32[4]{0:T(128)S(1)}, f32[4]{0:T(128)S(1)}) all-reduce(f32[4]{0:T(128)S(1)} %dynamic-update-slice.6, f32[4]{0:T(128)S(1)} %dynamic-update-slice.15, f32[4]{0:T(128)S(1)} %dynamic-update-slice.24), channel_id=1, replica_groups=mesh['dp'=8,'row_0'=2,'row_1'=4,'row_2'=2,'col'=4] {'row_1'}, use_global_device_ids=true, to_apply=%add.6 | all-reduce | flops 12 | bytes 96
  495.7 10.9 %all-reduce.29 = (f32[4]{0:T(128)S(1)}, f32[4]{0:T(128)S(1)}, f32[4]{0:T(128)S(1)}) all-reduce(f32[4]{0:T(128)S(1)} %dynamic-update-slice.8, f32[4]{0:T(128)S(1)} %dynamic-update-slice.17, f32[4]{0:T(128)S(1)} %dynamic-update-slice.26), channel_id=1, replica_groups=mesh['dp'=8,'row_0'=2,'row_1'=4,'row_2'=2,'col'=4] {'col'}, use_global_device_ids=true, to_apply=%add.8 | all-reduce | flops 12 | bytes 96
  515.4 25.0 %all-to-all-done.6 = bf16[8,32,1024]{2,1,0:T(8,128)(2,1)S(1)} async-done(((bf16[8,32,1024]{2,1,0:T(8,128)(2,1)}), bf16[8,32,1024]{2,1,0:T(8,128)(2,1)S(1)}, u32[]{:S(2)}, u32[]{:S(2)}) %all-to-all-start.6) | async-done | bytes 524320 | tf_op jit(solution)/shard_map/all_to_all | solution.py:30
  547.8 31.4 %all-to-all-done.4 = bf16[8,32,1280]{2,1,0:T(8,128)(2,1)S(1)} async-done(((bf16[8,32,1280]{2,1,0:T(8,128)(2,1)}), bf16[8,32,1280]{2,1,0:T(8,128)(2,1)S(1)}, u32[]{:S(2)}, u32[]{:S(2)}) %all-to-all-start.4) | async-done | bytes 655392 | tf_op jit(solution)/shard_map/all_to_all | solution.py:30
  584.4 33.5 %all-to-all-done.5 = bf16[8,40,1024]{2,1,0:T(8,128)(2,1)S(1)} async-done(((bf16[8,40,1024]{2,1,0:T(8,128)(2,1)}), bf16[8,40,1024]{2,1,0:T(8,128)(2,1)S(1)}, u32[]{:S(2)}, u32[]{:S(2)}) %all-to-all-start.5) | async-done | bytes 655392 | tf_op jit(solution)/shard_map/all_to_all | solution.py:30
  (197 shorter events, 122.9 us)
Async XLA Ops:
  6.7 13.7 %copy-start = (bf16[1,256,1280]{2,1,0:T(8,128)(2,1)S(1)}, bf16[1,256,1280]{2,1,0:T(8,128)(2,1)}, u32[]{:S(2)}) copy-start(bf16[1,256,1280]{2,1,0:T(8,128)(2,1)} %param.12) | copy-start | bytes 1966084
  7.9 41.3 %all-to-all-start.2 = ((bf16[8,2,16384]{2,1,0:T(2,128)(2,1)}), bf16[8,2,16384]{2,1,0:T(2,128)(2,1)S(1)}, u32[]{:S(2)}, u32[]{:S(2)}) async-start(bf16[8,2,16384]{2,1,0:T(2,128)(2,1)} %reshape.231), calls=%async_computation.2 | async-start | bytes 1048576 | tf_op jit(solution)/shard_map/all_to_all | solution.py:65
  27.1 26.4 %copy-start.1 = (bf16[1,320,1024]{2,1,0:T(8,128)(2,1)S(1)}, bf16[1,320,1024]{2,1,0:T(8,128)(2,1)}, u32[]{:S(2)}) copy-start(bf16[1,320,1024]{2,1,0:T(8,128)(2,1)} %param.16) | copy-start | bytes 1966084
  49.2 38.3 %all-to-all-start = ((bf16[8,2,20480]{2,1,0:T(2,128)(2,1)}), bf16[8,2,20480]{2,1,0:T(2,128)(2,1)S(1)}, u32[]{:S(2)}, u32[]{:S(2)}) async-start(bf16[8,2,20480]{2,1,0:T(2,128)(2,1)} %reshape.229), calls=%async_computation | async-start | bytes 1310720 | tf_op jit(solution)/shard_map/all_to_all | solution.py:65
  87.4 162.7 %all-to-all-start.1 = ((bf16[8,2,20480]{2,1,0:T(2,128)(2,1)}), bf16[8,2,20480]{2,1,0:T(2,128)(2,1)S(1)}, u32[]{:S(2)}, u32[]{:S(2)}) async-start(bf16[8,2,20480]{2,1,0:T(2,128)(2,1)} %reshape.233), calls=%async_computation.1 | async-start | bytes 1310720 | tf_op jit(solution)/shard_map/all_to_all | solution.py:65
  97.3 78.4 %copy-start.12 = (f32[1024]{0:T(1024)S(1)}, f32[1024]{0:T(1024)}, u32[]{:S(2)}) copy-start(f32[1024]{0:T(1024)} %param.23) | copy-start | bytes 12292
  175.7 332.2 %copy-start.6 = (f32[1024]{0:T(1024)}, f32[1024]{0:T(1024)S(1)}, u32[]{:S(2)}) copy-start(f32[1024]{0:T(1024)S(1)} %multiply_add_fusion.4) | copy-start | bytes 12292
  250.8 65.1 %copy-start.8 = (f32[1280]{0:T(1024)S(1)}, f32[1280]{0:T(1024)}, u32[]{:S(2)}) copy-start(f32[1280]{0:T(1024)} %param.15) | copy-start | bytes 15364
  250.8 77.2 %copy-start.14 = (f32[40]{0:T(128)S(1)}, f32[40]{0:T(128)}, u32[]{:S(2)}) copy-start(f32[40]{0:T(128)} %param.18) | copy-start | bytes 484
  250.8 77.9 %copy-start.15 = (f32[32]{0:T(128)S(1)}, f32[32]{0:T(128)}, u32[]{:S(2)}) copy-start(f32[32]{0:T(128)} %param.22) | copy-start | bytes 388
  250.9 77.8 %copy-start.16 = (f32[32]{0:T(128)S(1)}, f32[32]{0:T(128)}, u32[]{:S(2)}) copy-start(f32[32]{0:T(128)} %param.14) | copy-start | bytes 388
  250.9 155.5 %copy-start.13 = (f32[1024]{0:T(1024)S(1)}, f32[1024]{0:T(1024)}, u32[]{:S(2)}) copy-start(f32[1024]{0:T(1024)} %param.19) | copy-start | bytes 12292
  251.1 256.9 %copy-start.4 = (f32[32,1024]{1,0:T(8,128)S(1)}, f32[32,1024]{1,0:T(8,128)}, u32[]{:S(2)}) copy-start(f32[32,1024]{1,0:T(8,128)} %param.21) | copy-start | bytes 393220
  252.0 76.0 %all-to-all-start.3 = ((f32[4,1,104]{2,1,0:T(1,128)}), f32[4,1,104]{2,1,0:T(1,128)S(1)}, u32[]{:S(2)}, u32[]{:S(2)}) async-start(f32[4,1,104]{2,1,0:T(1,128)} %broadcast_in_dim.8), calls=%async_computation.3 | async-start | bytes 4096 | tf_op jit(solution)/shard_map/all_to_all | solution.py:30
  315.9 198.6 %copy-start.5 = (f32[1280]{0:T(1024)}, f32[1280]{0:T(1024)S(1)}, u32[]{:S(2)}) copy-start(f32[1280]{0:T(1024)S(1)} %multiply_add_fusion.3) | copy-start | bytes 15364
  328.7 218.2 %copy-start.9 = (f32[40]{0:T(128)}, f32[40]{0:T(128)S(1)}, u32[]{:S(2)}) copy-start(f32[40]{0:T(128)S(1)} %get-tuple-element.87) | copy-start | bytes 484
  329.4 180.3 %copy-start.11 = (f32[32]{0:T(128)}, f32[32]{0:T(128)S(1)}, u32[]{:S(2)}) copy-start(f32[32]{0:T(128)S(1)} %get-tuple-element.92) | copy-start | bytes 388
  329.4 185.1 %copy-start.10 = (f32[32]{0:T(128)}, f32[32]{0:T(128)S(1)}, u32[]{:S(2)}) copy-start(f32[32]{0:T(128)S(1)} %get-tuple-element.82) | copy-start | bytes 388
  406.4 140.6 %copy-start.7 = (f32[1024]{0:T(1024)}, f32[1024]{0:T(1024)S(1)}, u32[]{:S(2)}) copy-start(f32[1024]{0:T(1024)S(1)} %multiply_add_fusion.5) | copy-start | bytes 12292
  414.9 99.6 %copy-start.2 = (f32[32,1280]{1,0:T(8,128)S(1)}, f32[32,1280]{1,0:T(8,128)}, u32[]{:S(2)}) copy-start(f32[32,1280]{1,0:T(8,128)} %param.13) | copy-start | bytes 491524
  509.7 30.7 %all-to-all-start.6 = ((bf16[8,32,1024]{2,1,0:T(8,128)(2,1)}), bf16[8,32,1024]{2,1,0:T(8,128)(2,1)S(1)}, u32[]{:S(2)}, u32[]{:S(2)}) async-start(bf16[8,32,1024]{2,1,0:T(8,128)(2,1)} %broadcast_in_dim.21), calls=%async_computation.6 | async-start | bytes 1048576 | tf_op jit(solution)/shard_map/all_to_all | solution.py:30
  514.5 32.4 %copy-start.3 = (f32[40,1024]{1,0:T(8,128)S(1)}, f32[40,1024]{1,0:T(8,128)}, u32[]{:S(2)}) copy-start(f32[40,1024]{1,0:T(8,128)} %param.17) | copy-start | bytes 491524
  541.3 37.9 %all-to-all-start.4 = ((bf16[8,32,1280]{2,1,0:T(8,128)(2,1)}), bf16[8,32,1280]{2,1,0:T(8,128)(2,1)S(1)}, u32[]{:S(2)}, u32[]{:S(2)}) async-start(bf16[8,32,1280]{2,1,0:T(8,128)(2,1)} %broadcast_in_dim.9), calls=%async_computation.4 | async-start | bytes 1310720 | tf_op jit(solution)/shard_map/all_to_all | solution.py:30
  580.1 37.8 %all-to-all-start.5 = ((bf16[8,40,1024]{2,1,0:T(8,128)(2,1)}), bf16[8,40,1024]{2,1,0:T(8,128)(2,1)S(1)}, u32[]{:S(2)}, u32[]{:S(2)}) async-start(bf16[8,40,1024]{2,1,0:T(8,128)(2,1)} %broadcast_in_dim.20), calls=%async_computation.5 | async-start | bytes 1310720 | tf_op jit(solution)/shard_map/all_to_all | solution.py:30
